TPU v7x, 64 devices: a 2x2x8 block of a 4x4x8 slice. The times are simulated.
64 devices in a mesh: dp: 4 (over x, y), tp: 16 (over z, core).
Axes of the slice: x: 2, y: 2, z: 8, core: 2. Of those that a mesh axis runs over, the one named last changes fastest.
The devices are a block of a 4x4x8 slice.
Arguments:
- x: bfloat16 [2048, 3072], P(('dp', 'tp')), parts along dimension 0
- dy: bfloat16 [2048, 3072], P(('dp', 'tp')), parts along dimension 0
- wg: bfloat16 [3072, 8192], P(None, 'tp')
- wu: bfloat16 [3072, 8192], P(None, 'tp')
- wd: bfloat16 [8192, 3072], P('tp')
Outputs:
- output 1: bfloat16 [2048, 3072], P(('dp', 'tp')), parts along dimension 0
- output 2: float32 [12288, 8192], P('dp', 'tp'), parts along dimension 0
- output 3: float32 [12288, 8192], P('dp', 'tp'), parts along dimension 0
- output 4: float32 [32768, 3072], P(('dp', 'tp')), parts along dimension 0
There are 4 independent parts. A program takes and returns all parts, laid end to end along the dimension named above; an argument that names none is the same for every part.
All inputs are finite; a program needn't handle non-finite values.
Results may differ from a plain program's by a relative error of at most 0.016622.
Values are sent between devices in bfloat16 or wider.
A program may use at most 768 MiB of HBM per device.

v0:
```python
import jax
import jax.numpy as jnp
from jax import lax
from jax.sharding import PartitionSpec as P


def _silu_and_grad(u):
    s = jax.nn.sigmoid(u)
    return u * s, s * (1.0 + u * (1.0 - s))


def solution(mesh):
    f32 = jnp.float32
    bf16 = jnp.bfloat16

    def local(x, dy, wg, wu, wd):
        xg = lax.all_gather(x, "tp", axis=0, tiled=True)
        dyg = lax.all_gather(dy, "tp", axis=0, tiled=True)
        ug = jnp.dot(xg, wg, preferred_element_type=f32).astype(bf16).astype(f32)
        uu = jnp.dot(xg, wu, preferred_element_type=f32).astype(bf16).astype(f32)
        a, da = _silu_and_grad(ug)
        z = (a * uu).astype(bf16)
        dwd = jnp.dot(z.T, dyg, preferred_element_type=f32)
        g = jnp.dot(dyg, wd.T, preferred_element_type=f32)
        duu = (g * a).astype(bf16)
        dug = (g * uu * da).astype(bf16)
        p = jnp.dot(dug, wg.T, preferred_element_type=f32) + jnp.dot(duu, wu.T, preferred_element_type=f32)
        dx = lax.psum_scatter(p.astype(bf16), "tp", scatter_dimension=0, tiled=True)
        dwg = jnp.dot(xg.T, dug, preferred_element_type=f32)
        dwu = jnp.dot(xg.T, duu, preferred_element_type=f32)
        return dx, dwg, dwu, dwd

    rows = P(("dp", "tp"), None)
    return jax.shard_map(local, mesh=mesh,
                         in_specs=(rows, rows, P(None, "tp"), P(None, "tp"), P("tp", None)),
                         out_specs=(rows, P("dp", "tp"), P("dp", "tp"), rows),
                         check_vma=False)
```

profile of v0, /device:TPU:21, one launch (start us, length us, event | category | flops | bytes accessed | tf_op | source)
XLA Modules:
  0.0 161.0 jit_solution(630030560086263502)
XLA Ops:
  7.2 0.0 copy-start
  7.2 0.1 all-gather.5.cloned.1.call-start
  7.3 0.7 all-gather.5.cloned.1.call-update
  8.0 0.1 all-gather.3.cloned.1.call-start
  8.1 0.7 all-gather.3.cloned.1.call-update
  8.8 0.1 reduce-scatter.2.cloned.1.call-start
  8.9 43.4 %all-gather.5.cloned.1.call-done = bf16[512,3072]{1,0:T(8,128)(2,1)} async-done(((bf16[32,3072]{1,0:T(8,128)(2,1)}), bf16[512,3072]{1,0:T(8,128)(2,1)}) %all-gather.5.cloned.1.call-update) | async-done | bytes 3145744 | tf_op jit(solution)/shard_map/all_gather | solution.py:17
  52.2 4.6 %convolution_convert_fusion = bf16[512,512]{1,0:T(8,128)(2,1)} fusion(bf16[512,3072]{1,0:T(8,128)(2,1)} %all-gather.5.cloned.1.call-done, bf16[3072,512]{1,0:T(8,128)(2,1)S(1)} %copy-done), kind=kOutput, calls=%fused_computation.8 | convolution fusion | flops 1610874880 | bytes 6815744 | tf_op jit(solution)/shard_map/dot_general | solution.py:19
  56.9 2.6 %convolution_convert_fusion.1 = bf16[512,512]{1,0:T(8,128)(2,1)} fusion(bf16[512,3072]{1,0:T(8,128)(2,1)S(1)} %copy-done.1, bf16[3072,512]{1,0:T(8,128)(2,1)S(1)} %copy-done.4), kind=kOutput, calls=%fused_computation.9 | convolution fusion | flops 1610874880 | bytes 6815744 | tf_op jit(solution)/shard_map/dot_general | solution.py:20
  59.4 30.2 %all-gather.3.cloned.1.call-done = bf16[512,3072]{1,0:T(8,128)(2,1)} async-done(((bf16[32,3072]{1,0:T(8,128)(2,1)}), bf16[512,3072]{1,0:T(8,128)(2,1)}) %all-gather.3.cloned.1.call-update) | async-done | bytes 3145744 | tf_op jit(solution)/shard_map/all_gather | solution.py:18
  89.6 5.1 %fusion.1 = (bf16[512,512]{1,0:T(8,128)(2,1)S(1)}, f32[512,512]{1,0:T(8,128)S(1)}) fusion(bf16[512,512]{1,0:T(8,128)(2,1)} %convolution_convert_fusion.1, bf16[512,512]{1,0:T(8,128)(2,1)} %convolution_convert_fusion, bf16[512,3072]{1,0:T(8,128)(2,1)} %all-gather.3.cloned.1.call-done, bf16[512,3072]{1,0:T(8,128)(2,1)} %param.9), kind=kOutput, calls=%fused_computation.11 | convolution fusion | flops 1613758464 | bytes 8912896 | tf_op jit(solution)/shard_map/dot_general | solution.py:24
  94.8 0.0 copy-start.6
  94.8 0.0 copy-start.3
  94.8 0.0 copy-start.5
  94.8 1.8 %fusion.11 = f32[512,3072]{1,0:T(8,128)S(1)} fusion(bf16[512,512]{1,0:T(8,128)(2,1)S(1)} %get-tuple-element.8, bf16[3072,512]{1,0:T(8,128)(2,1)S(1)} %copy-done), kind=kOutput, calls=%fused_computation.21 | convolution fusion | flops 1610612736 | bytes 9961472 | tf_op jit(solution)/shard_map/dot_general | solution.py:27
  96.7 0.7 copy-done.5
  97.4 3.6 %add_convert_fusion = bf16[512,3072]{1,0:T(8,128)(2,1)} fusion(f32[512,3072]{1,0:T(8,128)S(1)} %fusion.11, bf16[3072,512]{1,0:T(8,128)(2,1)S(1)} %copy-done.5, f32[512,512]{1,0:T(8,128)S(1)} %get-tuple-element.9, bf16[512,512]{1,0:T(8,128)(2,1)S(1)} %copy-done.2), kind=kOutput, calls=%fused_computation | convolution fusion | flops 1615593472 | bytes 14155776 | tf_op jit(solution)/shard_map/dot_general | solution.py:27
  101.0 0.1 reduce-scatter.2.cloned.1.call-update
  101.1 7.0 %convolution_bitcast_fusion = f32[3072,512]{0,1:T(8,128)} fusion(bf16[512,3072]{1,0:T(8,128)(2,1)} %all-gather.5.cloned.1.call-done, f32[512,512]{1,0:T(8,128)} %copy-done.3, bf16[512,512]{1,0:T(8,128)(2,1)} %convolution_convert_fusion), kind=kOutput, calls=%fused_computation.1 | convolution fusion | flops 1612447744 | bytes 11010048 | tf_op jit(solution)/shard_map/dot_general | solution.py:30
  108.1 6.6 %copy.10 = f32[3072,512]{1,0:T(8,128)} copy(f32[3072,512]{0,1:T(8,128)} %convolution_bitcast_fusion) | data formatting | bytes 12582912
  114.6 6.6 %convolution_bitcast_fusion.1 = f32[3072,512]{0,1:T(8,128)} fusion(bf16[512,512]{1,0:T(8,128)(2,1)} %copy-done.6, bf16[512,3072]{1,0:T(8,128)(2,1)} %all-gather.5.cloned.1.call-done), kind=kOutput, calls=%fused_computation.2 | convolution fusion | flops 1610612736 | bytes 9961472 | tf_op jit(solution)/shard_map/dot_general | solution.py:29
  121.2 6.6 %copy.9 = f32[3072,512]{1,0:T(8,128)} copy(f32[3072,512]{0,1:T(8,128)} %convolution_bitcast_fusion.1) | data formatting | bytes 12582912
  127.8 6.8 %fusion.8 = f32[512,3072]{1,0:T(8,128)} fusion(bf16[512,3072]{1,0:T(8,128)(2,1)} %all-gather.3.cloned.1.call-done, bf16[512,512]{1,0:T(8,128)(2,1)} %convolution_convert_fusion.1, bf16[512,512]{1,0:T(8,128)(2,1)} %convolution_convert_fusion), kind=kOutput, calls=%fused_computation.19 | convolution fusion | flops 1612709888 | bytes 10485760 | tf_op jit(solution)/shard_map/dot_general | solution.py:23
  134.6 19.8 %reduce-scatter.2.cloned.1.call-done = bf16[32,3072]{1,0:T(8,128)(2,1)} async-done(((bf16[512,3072]{1,0:T(8,128)(2,1)}), bf16[32,3072]{1,0:T(8,128)(2,1)}) %reduce-scatter.2.cloned.1.call-update) | async-done | bytes 196624 | tf_op jit(solution)/shard_map/reduce_scatter | solution.py:28
  (9 shorter events, 0.0 us)
Async XLA Ops:
  7.2 45.0 %copy-start = (bf16[3072,512]{1,0:T(8,128)(2,1)S(1)}, bf16[3072,512]{1,0:T(8,128)(2,1)}, u32[]{:S(2)}) copy-start(bf16[3072,512]{1,0:T(8,128)(2,1)} %param.7) | copy-start | bytes 9437188
  7.2 45.0 %all-gather.5.cloned.1.call-start = ((), (), s32[]{:S(2)}) async-start(), calls=%async_computation.2 | async-start | bytes 3342336 | tf_op jit(solution)/shard_map/all_gather | solution.py:17
  8.0 81.7 %all-gather.3.cloned.1.call-start = ((), (), s32[]{:S(2)}) async-start(), calls=%async_computation.1 | async-start | bytes 3342336 | tf_op jit(solution)/shard_map/all_gather | solution.py:18
  8.8 145.6 %reduce-scatter.2.cloned.1.call-start = ((), (), s32[]{:S(2)}) async-start(), calls=%async_computation.3 | async-start | bytes 3342336 | tf_op jit(solution)/shard_map/reduce_scatter | solution.py:28
  52.2 4.6 %copy-start.1 = (bf16[512,3072]{1,0:T(8,128)(2,1)S(1)}, bf16[512,3072]{1,0:T(8,128)(2,1)}, u32[]{:S(2)}) copy-start(bf16[512,3072]{1,0:T(8,128)(2,1)} %all-gather.5.cloned.1.call-done) | copy-start | bytes 9437188
  52.2 4.6 %copy-start.4 = (bf16[3072,512]{1,0:T(8,128)(2,1)S(1)}, bf16[3072,512]{1,0:T(8,128)(2,1)}, u32[]{:S(2)}) copy-start(bf16[3072,512]{1,0:T(8,128)(2,1)} %param.8) | copy-start | bytes 9437188
  94.8 1.9 %copy-start.6 = (bf16[512,512]{1,0:T(8,128)(2,1)}, bf16[512,512]{1,0:T(8,128)(2,1)S(1)}, u32[]{:S(2)}) copy-start(bf16[512,512]{1,0:T(8,128)(2,1)S(1)} %get-tuple-element.8) | copy-start | bytes 1572868
  94.8 1.9 %copy-start.3 = (f32[512,512]{1,0:T(8,128)}, f32[512,512]{1,0:T(8,128)S(1)}, u32[]{:S(2)}) copy-start(f32[512,512]{1,0:T(8,128)S(1)} %get-tuple-element.9) | copy-start | bytes 3145732
  94.8 1.9 %copy-start.2 = (bf16[512,512]{1,0:T(8,128)(2,1)S(1)}, bf16[512,512]{1,0:T(8,128)(2,1)}, u32[]{:S(2)}) copy-start(bf16[512,512]{1,0:T(8,128)(2,1)} %convolution_convert_fusion) | copy-start | bytes 1572868
  94.8 2.6 %copy-start.5 = (bf16[3072,512]{1,0:T(8,128)(2,1)S(1)}, bf16[3072,512]{1,0:T(8,128)(2,1)}, u32[]{:S(2)}) copy-start(bf16[3072,512]{1,0:T(8,128)(2,1)} %param.8) | copy-start | bytes 9437188
Sparse Core Ops, SparseCore 0:
  9.7 42.5 all-gather.4
  53.8 35.7 all-gather.2
  101.2 53.1 reduce-scatter.1
where the time goes:
time: 163 us; the launch traced here: 161 us
  waiting for transfers between devices  94.9 us (58%)
  matrix products  38.2 us (23%)
  local copies, waits for them, and re-layouts  13.9 us (9%)
  between operations  13.9 us (9%)
    all_gather x1, waiting for transfers between devices, local(): xg = lax.all_gather(x, 'tp', axis=0, tiled=True)  43.4 us
    all_gather x1, waiting for transfers between devices, local(): dyg = lax.all_gather(dy, 'tp', axis=0, tiled=True)  30.2 us
    reduce_scatter x1, waiting for transfers between devices, local(): dx = lax.psum_scatter(p.astype(bf16), 'tp', scatter_dimension=0, tiled=True)  19.8 us
    unnamed x16, local copies, waits for them, and re-layouts  13.9 us
    dot_general x1, matrix products, local(): dwu = jnp.dot(xg.T, duu, preferred_element_type=f32)  6.98 us
    dot_general x1, matrix products, local(): dwd = jnp.dot(z.T, dyg, preferred_element_type=f32)  6.84 us
    dot_general x1, matrix products, local(): dwg = jnp.dot(xg.T, dug, preferred_element_type=f32)  6.59 us
    dot_general x1, matrix products, local(): g = jnp.dot(dyg, wd.T, preferred_element_type=f32)  5.1 us
  transfers between devices with their start and end apart: 3, of which 3 were waited for; matrix products, arithmetic and copies ran while one was open for 25% of the time, Pallas kernels for 0%

commit v1 on v0

v1 whole, which is shorter than its diff:
```python
import functools

import jax
import jax.numpy as jnp
from jax import lax
from jax.experimental import pallas as pl
from jax.experimental.pallas import tpu as pltpu
from jax.sharding import PartitionSpec as P

MESH = pl.DeviceIdType.MESH
F32 = jnp.float32
BF16 = jnp.bfloat16
CORES = 2
PIECES = 4
NT = (((1,), (1,)), ((), ()))


def _silu_and_grad(u):
    s = jax.nn.sigmoid(u)
    return u * s, s * (1.0 + u * (1.0 - s))


def _main_kernel(nz, rows, x_hbm, dy_hbm, wg_hbm, wu_hbm, wd_hbm,
                 dx_ref, xg_out, dyg_out, dug_out, duu_out, z_out,
                 xg, dyg, wg, wu, wd, dug, duu, zz, pown, psend, psib, rsend, rrecv,
                 own_sem, w_sem, ag_send, ag_recv, sib_send, sib_recv, ps_send, ps_recv,
                 rs_send, rs_recv, out_sem):
    far = nz // 2
    near = nz - 1 - far
    me = lax.axis_index("tp")
    z = me // CORES
    c = lax.rem(me, CORES)
    right = {"tp": lax.rem(z + 1, nz) * CORES + c}
    left = {"tp": lax.rem(z + nz - 1, nz) * CORES + c}
    sib = {"tp": z * CORES + (1 - c)}
    width = x_hbm.shape[1]
    pw = width // PIECES
    arrays = (xg, dyg)

    def chip(off):
        return lax.rem(z + off + 2 * nz, nz)

    own = [pltpu.make_async_copy(src, dst.at[z, 0], own_sem.at[i])
           for i, (src, dst) in enumerate(((x_hbm, xg), (dy_hbm, dyg)))]
    wcopies = [pltpu.make_async_copy(src, dst, w_sem.at[i])
               for i, (src, dst) in enumerate(((wg_hbm, wg), (wu_hbm, wu), (wd_hbm, wd)))]
    for cp in own:
        cp.start()
    for cp in wcopies:
        cp.start()
    barrier = pltpu.get_barrier_semaphore()
    for dev in (left, right, sib):
        pl.semaphore_signal(barrier, inc=1, device_id=dev, device_id_type=MESH)
    pl.semaphore_wait(barrier, 3)

    def ag_copy(a, d, s):
        src_chip = chip(1 - s) if d == 0 else chip(s - 1)
        blk = arrays[a].at[src_chip, 0]
        return pltpu.make_async_remote_copy(
            blk, blk, ag_send.at[a, d, s - 1], ag_recv.at[a, d, s - 1],
            device_id=right if d == 0 else left, device_id_type=MESH)

    def sib_copy(a, b):
        return pltpu.make_async_remote_copy(
            arrays[a].at[b, 0], arrays[a].at[b, 1], sib_send.at[a, b], sib_recv.at[a, b],
            device_id=sib, device_id_type=MESH)

    def psum_copy(b):
        return pltpu.make_async_remote_copy(
            psend.at[b], psib.at[b], ps_send.at[b], ps_recv.at[b], device_id=sib, device_id_type=MESH)

    def compute(b):
        for a in range(2):
            sib_copy(a, b).wait_recv()
        xb = xg[b].reshape(CORES * rows, width)
        dyb = dyg[b].reshape(CORES * rows, width)
        ug = jnp.dot(xb, wg[...], preferred_element_type=F32).astype(BF16).astype(F32)
        uu = jnp.dot(xb, wu[...], preferred_element_type=F32).astype(BF16).astype(F32)
        g = lax.dot_general(dyb, wd[...], NT, preferred_element_type=F32)
        a, da = _silu_and_grad(ug)
        zz[b] = (a * uu).astype(BF16)
        u = (g * a).astype(BF16)
        duu[b] = u
        v = (g * uu * da).astype(BF16)
        dug[b] = v
        for q in range(PIECES):
            cols = slice(q * pw, (q + 1) * pw)
            p = (lax.dot_general(v, wg[cols, :], NT, preferred_element_type=F32)
                 + lax.dot_general(u, wu[cols, :], NT, preferred_element_type=F32))
            pown[b, q] = p[:rows]
            psend[b, q] = p[rows:].astype(BF16)
        psum_copy(b).start()

    for a in range(2):
        own[a].wait()
        d0 = a
        ag_copy(a, d0, 1).start()
    for a in range(2):
        ag_copy(a, 1 - a, 1).start()
        sib_copy(a, z).start()
    for cp in wcopies:
        cp.wait()

    @pl.loop(1, far + 1)
    def _(s):
        for a in range(2):
            ag_copy(a, a, s).wait_recv()

            @pl.when(s < far)
            def _():
                ag_copy(a, a, s + 1).start()
            sib_copy(a, chip(-s) if a == 0 else chip(s)).start()
        compute(chip(s - 1))

        @pl.when(s <= near)
        def _():
            for a in range(2):
                ag_copy(a, 1 - a, s).wait_recv()

                @pl.when(s < near)
                def _():
                    ag_copy(a, 1 - a, s + 1).start()
                sib_copy(a, chip(s) if a == 0 else chip(-s)).start()
        compute(chip(-s))

    outs = [pltpu.make_async_copy(src, dst, out_sem.at[i]) for i, (src, dst) in enumerate(
        ((xg, xg_out), (dyg, dyg_out), (dug, dug_out), (duu, duu_out), (zz, z_out)))]
    for cp in outs:
        cp.start()

    def hops(d, q):
        return far if (q + d) % 2 == 0 else near

    def rs_copy(d, q, s):
        return pltpu.make_async_remote_copy(
            rsend.at[d, q, s], rrecv.at[d, q, s], rs_send.at[d, q, s], rs_recv.at[d, q, s],
            device_id=right if d == 0 else left, device_id_type=MESH)

    def partial(b, q):
        return pown[b, q] + psib[b, q].astype(F32)

    def rs_step(d, q, s):
        h = hops(d, q)
        b = chip(h - s) if d == 0 else chip(s - h)
        t = partial(b, q)
        if s > 0:
            rs_copy(d, q, s - 1).wait_recv()
            t = t + rrecv[d, q, s - 1].astype(F32)
        rsend[d, q, s] = t.astype(BF16)
        rs_copy(d, q, s).start()

    for off in range(nz):
        psum_copy(chip(off)).wait_recv()
    for s in range(far):
        for long in (False, True):
            for q in range(PIECES):
                for d in range(2):
                    if ((q + d) % 2 == 0) == long and s < hops(d, q):
                        rs_step(d, q, s)
    for q in range(PIECES):
        t = partial(z, q)
        for d in range(2):
            h = hops(d, q)
            rs_copy(d, q, h - 1).wait_recv()
            t = t + rrecv[d, q, h - 1].astype(F32)
        dx_ref[:, q * pw:(q + 1) * pw] = t.astype(BF16)

    for a in range(2):
        for d in range(2):
            for s in range(1, (far if a == d else near) + 1):
                ag_copy(a, d, s).wait_send()
        for off in range(nz):
            sib_copy(a, chip(off)).wait_send()
    for off in range(nz):
        psum_copy(chip(off)).wait_send()
    for d in range(2):
        for q in range(PIECES):
            for s in range(hops(d, q)):
                rs_copy(d, q, s).wait_send()
    for cp in outs:
        cp.wait()


def _grad_kernel(x_ref, dy_ref, dug_ref, duu_ref, z_ref, dwg_ref, dwu_ref, dwd_ref, zt):
    @pl.when(pl.program_id(0) == 0)
    def _():
        zt[...] = z_ref[...].T
    xt = x_ref[...].T
    dwg_ref[...] = jnp.dot(xt, dug_ref[...], preferred_element_type=F32)
    dwu_ref[...] = jnp.dot(xt, duu_ref[...], preferred_element_type=F32)
    dwd_ref[...] = jnp.dot(zt[...], dy_ref[...], preferred_element_type=F32)


def solution(mesh):
    n = mesh.shape["tp"]
    nz = n // CORES

    def local(x, dy, wg, wu, wd):
        rows, width = x.shape
        hid = wg.shape[1]
        tok = rows * n
        far = nz // 2
        pw = width // PIECES
        S = jax.ShapeDtypeStruct
        hbm = pl.BlockSpec(memory_space=pltpu.HBM)
        dma = pltpu.SemaphoreType.DMA
        dx, xg, dyg, dug, duu, z = pl.pallas_call(
            functools.partial(_main_kernel, nz, rows),
            out_shape=[S((rows, width), BF16)] + [S((nz, CORES, rows, width), BF16)] * 2
            + [S((nz, CORES * rows, hid), BF16)] * 3,
            in_specs=[hbm] * 5,
            out_specs=[pl.BlockSpec(memory_space=pltpu.VMEM)] + [hbm] * 5,
            scratch_shapes=[
                pltpu.VMEM((nz, CORES, rows, width), BF16),
                pltpu.VMEM((nz, CORES, rows, width), BF16),
                pltpu.VMEM((width, hid), BF16),
                pltpu.VMEM((width, hid), BF16),
                pltpu.VMEM((hid, width), BF16),
                pltpu.VMEM((nz, CORES * rows, hid), BF16),
                pltpu.VMEM((nz, CORES * rows, hid), BF16),
                pltpu.VMEM((nz, CORES * rows, hid), BF16),
                pltpu.VMEM((nz, PIECES, rows, pw), F32),
                pltpu.VMEM((nz, PIECES, rows, pw), BF16),
                pltpu.VMEM((nz, PIECES, rows, pw), BF16),
                pltpu.VMEM((2, PIECES, far, rows, pw), BF16),
                pltpu.VMEM((2, PIECES, far, rows, pw), BF16),
                dma((2,)), dma((3,)),
                dma((2, 2, far)), dma((2, 2, far)),
                dma((2, nz)), dma((2, nz)),
                dma((nz,)), dma((nz,)),
                dma((2, PIECES, far)), dma((2, PIECES, far)),
                dma((5,)),
            ],
            compiler_params=pltpu.CompilerParams(
                collective_id=0, has_side_effects=True, vmem_limit_bytes=56 * 1024 * 1024),
            cost_estimate=pl.CostEstimate(
                flops=2 * 5 * tok * width * hid, bytes_accessed=6 * width * hid, transcendentals=tok * hid),
            name="gather_compute_scatter",
        )(x, dy, wg, wu, wd)
        bw = 256
        whole = lambda i: (0, 0)
        dwg, dwu, dwd = pl.pallas_call(
            _grad_kernel,
            grid=(width // bw,),
            out_shape=[S((width, hid), F32), S((width, hid), F32), S((hid, width), F32)],
            in_specs=[pl.BlockSpec((tok, bw), lambda i: (0, i)), pl.BlockSpec((tok, bw), lambda i: (0, i)),
                      pl.BlockSpec((tok, hid), whole), pl.BlockSpec((tok, hid), whole),
                      pl.BlockSpec((tok, hid), whole)],
            out_specs=[pl.BlockSpec((bw, hid), lambda i: (i, 0)), pl.BlockSpec((bw, hid), lambda i: (i, 0)),
                       pl.BlockSpec((hid, bw), lambda i: (0, i))],
            scratch_shapes=[pltpu.VMEM((hid, tok), BF16)],
            compiler_params=pltpu.CompilerParams(vmem_limit_bytes=60 * 1024 * 1024),
            cost_estimate=pl.CostEstimate(
                flops=2 * 3 * tok * width * hid, bytes_accessed=12 * width * hid + 4 * tok * width, transcendentals=0),
            name="weight_grads",
        )(xg.reshape(tok, width), dyg.reshape(tok, width), dug.reshape(tok, hid), duu.reshape(tok, hid),
          z.reshape(tok, hid))
        return dx, dwg, dwu, dwd

    rows = P(("dp", "tp"), None)
    return jax.shard_map(local, mesh=mesh,
                         in_specs=(rows, rows, P(None, "tp"), P(None, "tp"), P("tp", None)),
                         out_specs=(rows, P("dp", "tp"), P("dp", "tp"), rows),
                         check_vma=False)
```

time: 163 us -> 91.4 us (0.56)
  the two profiles are of different devices: /device:TPU:21 before, /device:TPU:28 now
where the time goes in v1:
time: 91.4 us; the launch traced here: 91 us
  Pallas kernels  89.7 us (98%)
    pallas_call x1, Pallas kernels, local(): pl.pallas_call(functools.partial(_main_kernel, nz, rows), out_shape=[S((r...  75.4 us
    pallas_call x1, Pallas kernels, local(): pl.pallas_call(_grad_kernel, grid=(width // bw,), out_shape=[S((width, hi...  14.3 us

profile of v1, /device:TPU:28, one launch (start us, length us, event | category | flops | bytes accessed | tf_op | source)
XLA Modules:
  0.0 91.0 jit_solution(10635617080291770753)
XLA Ops:
  0.6 75.4 %gather_compute_scatter.1 = (bf16[32,3072]{1,0:T(8,128)(2,1)}, bf16[8,2,32,3072]{3,2,1,0:T(8,128)(2,1)}, bf16[8,2,32,3072]{3,2,1,0:T(8,128)(2,1)}, bf16[8,64,512...) custom-call(bf16[32,3072]{1,0:T(8,128)(2,1)} %x_hbm.1, bf16[32,3072]{1,0:T(8,128)(2,1)} %dy_hbm.1, ...), custom_call_target="tpu_custom_call" | custom-call | flops 8053063680 | bytes 9437184 | tf_op jit(solution)/shard_map/gather_compute_scatter/pallas_call | solution.py:207
  76.1 0.0 copy-start
  76.1 14.3 %weight_grads.1 = (f32[3072,512]{1,0:T(8,128)}, f32[3072,512]{1,0:T(8,128)}, f32[512,3072]{1,0:T(8,128)}) custom-call(bf16[512,3072]{1,0:T(8,128)(2,1)} %bitcast.5, bf16[512,3072]{1,0:T(8,128)(2,1)} %bitcast.6, bf16[512,512]{1,0:T(8,128)(2,1)} %bitcast.7, bf16[512,512]{1,0:T(8,128)(2,1)} %bitcast.8, bf16[512,512]{1,0:T(8,128)(2,1)} %bitcast.9), custom_call_target="tpu_custom_call" | custom-call | flops 4831838208 | bytes 25165824 | tf_op jit(solution)/shard_map/weight_grads/pallas_call | solution.py:242
  90.4 0.0 copy-done
  90.4 0.7 copy.10
Async XLA Ops:
  76.1 14.3 %copy-start = (bf16[32,3072]{1,0:T(8,128)(2,1)S(1)}, bf16[32,3072]{1,0:T(8,128)(2,1)}, u32[]{:S(2)}) copy-start(bf16[32,3072]{1,0:T(8,128)(2,1)} %get-tuple-element.26) | copy-start | bytes 589828

commit v2 on v1

v2 whole, which is shorter than its diff:
```python
import functools

import jax
import jax.numpy as jnp
from jax import lax
from jax.experimental import pallas as pl
from jax.experimental.pallas import tpu as pltpu
from jax.sharding import PartitionSpec as P

MESH = pl.DeviceIdType.MESH
F32 = jnp.float32
BF16 = jnp.bfloat16
CORES = 2
PIECES = 4
NT = (((1,), (1,)), ((), ()))


def _silu_and_grad(u):
    s = jax.nn.sigmoid(u)
    return u * s, s * (1.0 + u * (1.0 - s))


def _main_kernel(nz, rows, x_hbm, dy_hbm, wg_hbm, wu_hbm, wd_hbm,
                 dx_ref, xg, dug, dwu_ref, dwd_ref,
                 dyg, duu, zz, zt, wg, wu, wd, wgt, wut, wdt, pown, psend, psib, rsend, rrecv,
                 own_sem, w_sem, ag_send, ag_recv, sib_send, sib_recv, ps_send, ps_recv,
                 rs_send, rs_recv):
    far = nz // 2
    near = nz - 1 - far
    me = lax.axis_index("tp")
    z = me // CORES
    c = lax.rem(me, CORES)
    right = {"tp": lax.rem(z + 1, nz) * CORES + c}
    left = {"tp": lax.rem(z + nz - 1, nz) * CORES + c}
    sib = {"tp": z * CORES + (1 - c)}
    width = x_hbm.shape[1]
    pw = width // PIECES
    blk = CORES * rows
    arrays = (xg, dyg)

    def chip(off):
        return lax.rem(z + off + 2 * nz, nz)

    own = [pltpu.make_async_copy(src, dst.at[z, 0], own_sem.at[i])
           for i, (src, dst) in enumerate(((x_hbm, xg), (dy_hbm, dyg)))]
    wcopies = [pltpu.make_async_copy(src, dst, w_sem.at[i])
               for i, (src, dst) in enumerate(((wg_hbm, wg), (wu_hbm, wu), (wd_hbm, wd)))]
    for cp in own:
        cp.start()
    for cp in wcopies:
        cp.start()
    barrier = pltpu.get_barrier_semaphore()
    for dev in (left, right, sib):
        pl.semaphore_signal(barrier, inc=1, device_id=dev, device_id_type=MESH)
    pl.semaphore_wait(barrier, 3)

    def ag_copy(a, d, s):
        src_chip = chip(1 - s) if d == 0 else chip(s - 1)
        part = arrays[a].at[src_chip, 0]
        return pltpu.make_async_remote_copy(
            part, part, ag_send.at[a, d, s - 1], ag_recv.at[a, d, s - 1],
            device_id=right if d == 0 else left, device_id_type=MESH)

    def sib_copy(a, b):
        return pltpu.make_async_remote_copy(
            arrays[a].at[b, 0], arrays[a].at[b, 1], sib_send.at[a, b], sib_recv.at[a, b],
            device_id=sib, device_id_type=MESH)

    def psum_copy(b, q):
        return pltpu.make_async_remote_copy(
            psend.at[b, q], psib.at[b, q], ps_send.at[b, q], ps_recv.at[b, q], device_id=sib, device_id_type=MESH)

    def stack(parts):
        return parts[0] if len(parts) == 1 else jnp.concatenate(parts, axis=0)

    def compute(bs):
        for b in bs:
            for a in range(2):
                sib_copy(a, b).wait_recv()
        xb = stack([xg[b].reshape(blk, width) for b in bs])
        dyb = stack([dyg[b].reshape(blk, width) for b in bs])
        ug = jnp.dot(xb, wg[...], preferred_element_type=F32).astype(BF16).astype(F32)
        uu = jnp.dot(xb, wu[...], preferred_element_type=F32).astype(BF16).astype(F32)
        g = jnp.dot(dyb, wdt[...], preferred_element_type=F32)
        a, da = _silu_and_grad(ug)
        zv = (a * uu).astype(BF16)
        u = (g * a).astype(BF16)
        v = (g * uu * da).astype(BF16)
        for i, b in enumerate(bs):
            part = slice(i * blk, (i + 1) * blk)
            zz[b] = zv[part]
            duu[b] = u[part]
            dug[b] = v[part]
        for q in range(PIECES):
            cols = slice(q * pw, (q + 1) * pw)
            p = (jnp.dot(v, wgt[:, cols], preferred_element_type=F32)
                 + jnp.dot(u, wut[:, cols], preferred_element_type=F32))
            for i, b in enumerate(bs):
                pown[b, q] = p[i * blk:i * blk + rows]
                psend[b, q] = p[i * blk + rows:(i + 1) * blk].astype(BF16)
                psum_copy(b, q).start()

    def hops(d, q):
        return far if (q + d) % 2 == 0 else near

    def rs_copy(d, q, s):
        return pltpu.make_async_remote_copy(
            rsend.at[d, q, s], rrecv.at[d, q, s], rs_send.at[d, q, s], rs_recv.at[d, q, s],
            device_id=right if d == 0 else left, device_id_type=MESH)

    def partial(b, q):
        psum_copy(b, q).wait_recv()
        return pown[b, q] + psib[b, q].astype(F32)

    def rs_round(s, h):
        for q in range(PIECES):
            for d in range(2):
                if hops(d, q) == h and s < h:
                    t = partial(chip(h - s) if d == 0 else chip(s - h), q)
                    if s > 0:
                        rs_copy(d, q, s - 1).wait_recv()
                        t = t + rrecv[d, q, s - 1].astype(F32)
                    rsend[d, q, s] = t.astype(BF16)
                    rs_copy(d, q, s).start()

    def grad_chunk(i, n):
        tok, w = nz * blk, width // n
        part = slice(i * w, (i + 1) * w)
        if i == 0:
            zt[...] = zz[...].reshape(tok, zz.shape[2]).T
        dwd_ref[:, part] = jnp.dot(zt[...], dyg[:, :, :, part].reshape(tok, w), preferred_element_type=F32)
        xt = xg[:, :, :, part].reshape(tok, w).T
        dwu_ref[part, :] = jnp.dot(xt, duu[...].reshape(tok, duu.shape[2]), preferred_element_type=F32)

    for a in range(2):
        own[a].wait()
        ag_copy(a, a, 1).start()
    for a in range(2):
        ag_copy(a, 1 - a, 1).start()
        sib_copy(a, z).start()
    for cp, w, wt in zip(wcopies, (wg, wu, wd), (wgt, wut, wdt)):
        cp.wait()
        wt[...] = w[...].T
    compute([z])

    def first_arrivals(s, forward):
        for a in range(2):
            ag_copy(a, a, s).wait_recv()
            if forward:
                ag_copy(a, a, s + 1).start()
            sib_copy(a, chip(-s) if a == 0 else chip(s)).start()

    @pl.loop(1, near + 1)
    def _(s):
        first_arrivals(s, True)
        for a in range(2):
            ag_copy(a, 1 - a, s).wait_recv()

            @pl.when(s < near)
            def _():
                ag_copy(a, 1 - a, s + 1).start()
            sib_copy(a, chip(s) if a == 0 else chip(-s)).start()
        compute([chip(s), chip(-s)])

    first_arrivals(far, False)
    rs_round(0, near)
    compute([chip(far)])
    for s in range(1, far + 1):
        rs_round(s - 1, far)
        rs_round(s, near)
        if s < far:
            grad_chunk(s - 1, far - 1)
    for q in range(PIECES):
        t = partial(z, q)
        for d in range(2):
            h = hops(d, q)
            rs_copy(d, q, h - 1).wait_recv()
            t = t + rrecv[d, q, h - 1].astype(F32)
        dx_ref[:, q * pw:(q + 1) * pw] = t.astype(BF16)

    for a in range(2):
        for d in range(2):
            for s in range(1, (far if a == d else near) + 1):
                ag_copy(a, d, s).wait_send()
        for off in range(nz):
            sib_copy(a, chip(off)).wait_send()
    for off in range(nz):
        for q in range(PIECES):
            psum_copy(chip(off), q).wait_send()
    for d in range(2):
        for q in range(PIECES):
            for s in range(hops(d, q)):
                rs_copy(d, q, s).wait_send()


def _grad_kernel(bw, x_ref, dug_ref, dx_vmem, dwu_vmem, dwd_vmem, dx_ref, dwg_ref, dwu_ref, dwd_ref, buf, done_sem, sem):
    steps = x_ref.shape[1] // bw
    stores = [pltpu.make_async_copy(src, dst, done_sem.at[i]) for i, (src, dst) in enumerate(
        ((dwd_vmem, dwd_ref), (dwu_vmem, dwu_ref), (dx_vmem, dx_ref)))]
    for cp in stores:
        cp.start()
    for i in range(steps):
        part = slice(i * bw, (i + 1) * bw)
        buf[part] = jnp.dot(x_ref[:, part].T, dug_ref[...], preferred_element_type=F32)
        stores.append(pltpu.make_async_copy(buf.at[part], dwg_ref.at[part], sem.at[i]))
        stores[-1].start()
    for cp in stores:
        cp.wait()


def solution(mesh):
    n = mesh.shape["tp"]
    nz = n // CORES

    def local(x, dy, wg, wu, wd):
        x, dy, wg, wu, wd = (pltpu.with_memory_space_constraint(v, pltpu.HBM) for v in (x, dy, wg, wu, wd))
        rows, width = x.shape
        hid = wg.shape[1]
        tok = rows * n
        far = nz // 2
        pw = width // PIECES
        S = jax.ShapeDtypeStruct
        hbm = pl.BlockSpec(memory_space=pltpu.HBM)
        dma = pltpu.SemaphoreType.DMA
        vmem = pl.BlockSpec(memory_space=pltpu.VMEM)
        dx, xg, dug, dwu, dwd = pl.pallas_call(
            functools.partial(_main_kernel, nz, rows),
            out_shape=[S((rows, width), BF16), S((nz, CORES, rows, width), BF16),
                       S((nz, CORES * rows, hid), BF16), S((width, hid), F32), S((hid, width), F32)],
            in_specs=[hbm] * 5,
            out_specs=[vmem] * 5,
            scratch_shapes=[
                pltpu.VMEM((nz, CORES, rows, width), BF16),
                pltpu.VMEM((nz, CORES * rows, hid), BF16),
                pltpu.VMEM((nz, CORES * rows, hid), BF16),
                pltpu.VMEM((hid, tok), BF16),
                pltpu.VMEM((width, hid), BF16),
                pltpu.VMEM((width, hid), BF16),
                pltpu.VMEM((hid, width), BF16),
                pltpu.VMEM((hid, width), BF16),
                pltpu.VMEM((hid, width), BF16),
                pltpu.VMEM((width, hid), BF16),
                pltpu.VMEM((nz, PIECES, rows, pw), F32),
                pltpu.VMEM((nz, PIECES, rows, pw), BF16),
                pltpu.VMEM((nz, PIECES, rows, pw), BF16),
                pltpu.VMEM((2, PIECES, far, rows, pw), BF16),
                pltpu.VMEM((2, PIECES, far, rows, pw), BF16),
                dma((2,)), dma((3,)),
                dma((2, 2, far)), dma((2, 2, far)),
                dma((2, nz)), dma((2, nz)),
                dma((nz, PIECES)), dma((nz, PIECES)),
                dma((2, PIECES, far)), dma((2, PIECES, far)),
            ],
            compiler_params=pltpu.CompilerParams(
                collective_id=0, has_side_effects=True, vmem_limit_bytes=36 * 1024 * 1024),
            cost_estimate=pl.CostEstimate(
                flops=2 * 5 * tok * width * hid, bytes_accessed=6 * width * hid, transcendentals=tok * hid),
            name="gather_compute_scatter",
        )(x, dy, wg, wu, wd)
        bw = 512
        dx, dwg, dwu, dwd = pl.pallas_call(
            functools.partial(_grad_kernel, bw),
            out_shape=[S((rows, width), BF16), S((width, hid), F32), S((width, hid), F32), S((hid, width), F32)],
            in_specs=[vmem] * 5,
            out_specs=[hbm] * 4,
            scratch_shapes=[pltpu.VMEM((width, hid), F32), dma((3,)), dma((width // bw,))],
            compiler_params=pltpu.CompilerParams(vmem_limit_bytes=16 * 1024 * 1024),
            cost_estimate=pl.CostEstimate(
                flops=2 * tok * width * hid, bytes_accessed=12 * width * hid, transcendentals=0),
            name="weight_grads",
        )(xg.reshape(tok, width), dug.reshape(tok, hid), dx, dwu, dwd)
        return dx, dwg, dwu, dwd

    rows = P(("dp", "tp"), None)
    return jax.shard_map(local, mesh=mesh,
                         in_specs=(rows, rows, P(None, "tp"), P(None, "tp"), P("tp", None)),
                         out_specs=(rows, P("dp", "tp"), P("dp", "tp"), rows),
                         check_vma=False)
```

time: 91.4 us -> 73.2 us (0.80)
  the two profiles are of different devices: /device:TPU:28 before, /device:TPU:21 now
where the time goes in v2:
time: 73.2 us; the launch traced here: 73.1 us
  Pallas kernels  72.3 us (99%)
  between operations  0.8 us (1%)
    pallas_call x1, Pallas kernels, local(): pl.pallas_call(functools.partial(_main_kernel, nz, rows), out_shape=[S((r...  65.1 us
    pallas_call x1, Pallas kernels, local(): pl.pallas_call(functools.partial(_grad_kernel, bw), out_shape=[S((rows, w...  7.21 us

profile of v2, /device:TPU:21, one launch (start us, length us, event | category | flops | bytes accessed | tf_op | source)
XLA Modules:
  0.0 73.1 jit_solution(14211078328620805425)
XLA Ops:
  0.6 65.1 %gather_compute_scatter.1 = (bf16[32,3072]{1,0:T(8,128)(2,1)S(1)}, bf16[8,2,32,3072]{3,2,1,0:T(8,128)(2,1)S(1)}, bf16[8,64,512]{2,1,0:T(8,128)(2,1)S(1)}, f32[3072,512]{1,0:T(8,128)S(1)}, f32[512,3072]{1,0:T(8,128)S(1)}) custom-call(bf16[32,3072]{1,0:T(8,128)(2,1)} %x_hbm.1, bf16[32,3072]{1,0:T(8,128)(2,1)} %dy_hbm.1, bf16[3072,512]{1,0:T(8,128)(2,1)} %wg_hbm.1, ...), custom_call_target="tpu_custom_call" | custom-call | flops 8053063680 | bytes 9437184 | tf_op jit(solution)/shard_map/gather_compute_scatter/pallas_call | solution.py:226
  65.8 7.2 %weight_grads.1 = (bf16[32,3072]{1,0:T(8,128)(2,1)}, f32[3072,512]{1,0:T(8,128)}, f32[3072,512]{1,0:T(8,128)}, f32[512,3072]{1,0:T(8,128)}) custom-call(bf16[512,3072]{1,0:T(8,128)(2,1)S(1)} %bitcast.2, bf16[512,512]{1,0:T(8,128)(2,1)S(1)} %bitcast.3, bf16[32,3072]{1,0:T(8,128)(2,1)S(1)} %get-tuple-element.11.dx_vmem, ...), custom_call_target="tpu_custom_call" | custom-call | flops 1610612736 | bytes 18874368 | tf_op jit(solution)/shard_map/weight_grads/pallas_call | solution.py:261

commit v3 on v2

v3 whole, which is shorter than its diff:
```python
import functools

import jax
import jax.numpy as jnp
from jax import lax
from jax.experimental import pallas as pl
from jax.experimental.pallas import tpu as pltpu
from jax.sharding import PartitionSpec as P

MESH = pl.DeviceIdType.MESH
F32 = jnp.float32
BF16 = jnp.bfloat16
CORES = 2
PIECES = 4
NT = (((1,), (1,)), ((), ()))


def _silu_and_grad(u):
    s = jax.nn.sigmoid(u)
    return u * s, s * (1.0 + u * (1.0 - s))


def _main_kernel(nz, rows, x_hbm, dy_hbm, wg_hbm, wu_hbm, wd_hbm,
                 dx_ref, xg, dug, dwu_ref, dwd_ref,
                 dyg, duu, zz, zt, wg, wu, wd, wgt, wut, wdt,
                 pown, psend, psib, own_sum, own_send, own_sib, rsend, rrecv, fin,
                 own_sem, w_sem, ag_send, ag_recv, sib_send, sib_recv, ps_send, ps_recv, os_send, os_recv,
                 rs_send, rs_recv, fin_send, fin_recv):
    far = nz // 2
    near = nz - 1 - far
    me = lax.axis_index("tp")
    z = me // CORES
    c = lax.rem(me, CORES)
    width = x_hbm.shape[1]
    pw = width // PIECES
    blk = CORES * rows
    arrays = (xg, dyg)

    def dev(step, core):
        return {"tp": lax.rem(z + step + nz, nz) * CORES + core}

    def slot(off):
        return lax.rem(off + 2 * nz, nz)

    def step_of(d):
        return 1 if d == 0 else -1

    own = [pltpu.make_async_copy(src, dst.at[0, c], own_sem.at[i])
           for i, (src, dst) in enumerate(((x_hbm, xg), (dy_hbm, dyg)))]
    wcopies = [pltpu.make_async_copy(src, dst, w_sem.at[i])
               for i, (src, dst) in enumerate(((wg_hbm, wg), (wu_hbm, wu), (wd_hbm, wd)))]
    for cp in own:
        cp.start()
    for cp in wcopies:
        cp.start()
    barrier = pltpu.get_barrier_semaphore()
    peers = [dev(0, 1 - c), dev(1, c), dev(-1, c), dev(1, 1 - c), dev(-1, 1 - c)]
    for peer in peers:
        pl.semaphore_signal(barrier, inc=1, device_id=peer, device_id_type=MESH)
    pl.semaphore_wait(barrier, len(peers))

    def ag_copy(a, d, s):
        off = 1 - s if d == 0 else s - 1
        return pltpu.make_async_remote_copy(
            arrays[a].at[slot(off), c], arrays[a].at[slot(off - step_of(d)), c],
            ag_send.at[a, d, s - 1], ag_recv.at[a, d, s - 1], device_id=dev(step_of(d), c), device_id_type=MESH)

    def far_copy(a, d):
        off = 1 - far if d == 0 else far - 1
        cols = pl.ds(d * (width // 2), width // 2)
        return pltpu.make_async_remote_copy(
            arrays[a].at[slot(off), c, :, cols], arrays[a].at[far, c, :, cols],
            ag_send.at[a, d, far - 1], ag_recv.at[a, d, far - 1], device_id=dev(step_of(d), c), device_id_type=MESH)

    def sib_copy(a, o):
        return pltpu.make_async_remote_copy(
            arrays[a].at[o, c], arrays[a].at[o, c], sib_send.at[a, o], sib_recv.at[a, o],
            device_id=dev(0, 1 - c), device_id_type=MESH)

    def sib_wait(a, o):
        pltpu.make_async_remote_copy(
            arrays[a].at[o, 1 - c], arrays[a].at[o, 1 - c], sib_send.at[a, o], sib_recv.at[a, o],
            device_id=dev(0, 1 - c), device_id_type=MESH).wait_recv()

    FAR = "far"

    def kept(o, q):
        if o is FAR:
            return (far if q % 2 == 0 else 0), q // 2
        return o, q // 2

    def psum_copy(o, q):
        k = kept(o, q)
        return pltpu.make_async_remote_copy(
            psend.at[k], psib.at[k], ps_send.at[k], ps_recv.at[k], device_id=dev(0, 1 - c), device_id_type=MESH)

    def own_copy(q):
        return pltpu.make_async_remote_copy(
            own_send.at[q], own_sib.at[q], os_send.at[q], os_recv.at[q], device_id=dev(0, 1 - c), device_id_type=MESH)

    def stack(ref, offs):
        parts = [ref[o].reshape(blk, ref.shape[-1]) for o in offs]
        return parts[0] if len(parts) == 1 else jnp.concatenate(parts, axis=0)

    def unstack(ref, offs, v):
        for i, o in enumerate(offs):
            ref[o] = v[i * blk:(i + 1) * blk]

    def x_part(offs):
        for o in offs:
            sib_wait(0, o)
        xb = stack(xg, offs)
        unstack(dug, offs, jnp.dot(xb, wg[...], preferred_element_type=F32).astype(BF16))
        unstack(duu, offs, jnp.dot(xb, wu[...], preferred_element_type=F32).astype(BF16))

    def y_part(offs, kind):
        for o in offs:
            sib_wait(1, o)
        g = jnp.dot(stack(dyg, offs), wdt[...], preferred_element_type=F32)
        ug = stack(dug, offs).astype(F32)
        uu = stack(duu, offs).astype(F32)
        a, da = _silu_and_grad(ug)
        unstack(zz, offs, (a * uu).astype(BF16))
        u = (g * a).astype(BF16)
        v = (g * uu * da).astype(BF16)
        unstack(duu, offs, u)
        unstack(dug, offs, v)
        for q in range(PIECES):
            cols = slice(q * pw, (q + 1) * pw)
            p = (jnp.dot(v, wgt[:, cols], preferred_element_type=F32)
                 + jnp.dot(u, wut[:, cols], preferred_element_type=F32))
            if kind == "own":
                own_sum[q] = jnp.where(c == 0, p[:rows], p[rows:])
                own_send[q] = jnp.where(c == 0, p[rows:], p[:rows]).astype(BF16)
                own_copy(q).start()
            elif kind == "far":
                pown[kept(FAR, q)] = p
                psend[kept(FAR, q)] = p.astype(BF16)

                @pl.when(c == 0)
                def _():
                    psum_copy(FAR, q).start()
            else:
                first = c if q % 2 == 0 else 1 - c
                keep_o = offs[1] + first * (offs[0] - offs[1])
                send_o = offs[0] + offs[1] - keep_o
                pown[kept(keep_o, q)] = jnp.where(first == 1, p[:blk], p[blk:])
                psend[kept(send_o, q)] = jnp.where(first == 1, p[blk:], p[:blk]).astype(BF16)
                psum_copy(send_o, q).start()

    def hops(d, q):
        return far if (q + d) % 2 == 0 else near

    def rs_copy(d, q, s):
        k = (d, q // 2, s)
        return pltpu.make_async_remote_copy(
            rsend.at[k], rrecv.at[k], rs_send.at[k], rs_recv.at[k], device_id=dev(step_of(d), c), device_id_type=MESH)

    def fin_copy(d, q, h):
        return pltpu.make_async_remote_copy(
            rsend.at[d, q // 2, hops(d, q) - 1, pl.ds(h * rows, rows)], fin.at[d, q],
            fin_send.at[d, q // 2, h], fin_recv.at[d, q], device_id=dev(step_of(d), h), device_id_type=MESH)

    def rs_round(s, n):
        for q in range(PIECES):
            for d in range(2):
                if hops(d, q) != n:
                    continue
                o = (n - s if d == 0 else s - n) % nz
                o = FAR if o == far else o
                psum_copy(o, q).wait_recv()
                t = pown[kept(o, q)] + psib[kept(o, q)].astype(F32)
                if s > 0:
                    rs_copy(d, q, s - 1).wait_recv()
                    t = t + rrecv[d, q // 2, s - 1].astype(F32)
                rsend[d, q // 2, s] = t.astype(BF16)
                if s < n - 1:
                    rs_copy(d, q, s).start()
                else:
                    for h in range(CORES):
                        fin_copy(d, q, h).start()

    def rs_drain(n):
        for d in range(2):
            for q in range(PIECES):
                if hops(d, q) == n:
                    for s in range(n - 1):
                        rs_copy(d, q, s).wait_send()
                    for h in range(CORES):
                        fin_copy(d, q, h).wait_send()

    def grad_chunk(i, n):
        tok, w = nz * blk, width // n
        part = slice(i * w, (i + 1) * w)
        if i == 0:
            zt[...] = zz[...].reshape(tok, zz.shape[2]).T
        dwd_ref[:, part] = jnp.dot(zt[...], dyg[:, :, :, part].reshape(tok, w), preferred_element_type=F32)
        xt = xg[:, :, :, part].reshape(tok, w).T
        dwu_ref[part, :] = jnp.dot(xt, duu[...].reshape(tok, duu.shape[2]), preferred_element_type=F32)

    for a in range(2):
        own[a].wait()
        for d in range(2):
            ag_copy(a, d, 1).start()
        sib_copy(a, 0).start()
    for cp, w, wt in zip(wcopies, (wg, wu, wd), (wgt, wut, wdt)):
        cp.wait()
        wt[...] = w[...].T
    def event(a, s):
        for d in range(2):
            ag_copy(a, d, s).wait_recv()
            if isinstance(s, int):
                (ag_copy(a, d, s + 1) if s < near else far_copy(a, d)).start()
            else:
                @pl.when(s < near)
                def _():
                    ag_copy(a, d, s + 1).start()

                @pl.when(s == near)
                def _():
                    far_copy(a, d).start()
            sib_copy(a, nz - s if d == 0 else s).start()

    def far_event(a):
        for d in range(2):
            far_copy(a, d).wait_recv()
        sib_copy(a, far).start()

    x_part([0])
    event(0, 1)
    y_part([0], "own")
    event(1, 1)
    x_part([1, nz - 1])

    @pl.loop(2, near + 1)
    def _(s):
        event(0, s)
        y_part([s - 1, nz + 1 - s], "pair")
        event(1, s)
        x_part([s, nz - s])

    far_event(0)
    y_part([near, nz - near], "pair")
    far_event(1)

    x_part([far])

    @pl.when(c == 0)
    def _():
        rs_round(0, near)
    y_part([far], "far")

    @pl.when(c == 1)
    def _():
        for s in range(far):
            rs_round(s, far)
            if s < far - 1:
                grad_chunk(s, far - 1)
        rs_drain(far)

    @pl.when(c == 0)
    def _():
        for s in range(1, near):
            rs_round(s, near)
            grad_chunk(s - 1, near)
        grad_chunk(near - 1, near)
        rs_drain(near)

    for q in range(PIECES):
        own_copy(q).wait_recv()
        t = own_sum[q] + own_sib[q].astype(F32)
        for d in range(2):
            fin_copy(d, q, 0).wait_recv()
            t = t + fin[d, q].astype(F32)
        dx_ref[:, q * pw:(q + 1) * pw] = t.astype(BF16)

    for a in range(2):
        for d in range(2):
            for s in range(1, far):
                ag_copy(a, d, s).wait_send()
            far_copy(a, d).wait_send()
        for o in range(nz):
            sib_copy(a, o).wait_send()
    for q in range(PIECES):
        own_copy(q).wait_send()
    for o in range(1, nz):
        if o != far:
            for q in range(0, PIECES, 2):
                psum_copy(o, q).wait_send()

    @pl.when(c == 0)
    def _():
        for q in range(PIECES):
            psum_copy(FAR, q).wait_send()


def _grad_kernel(bw, x_ref, dug_ref, dx_vmem, dwu_vmem, dwd_vmem, dx_ref, dwg_ref, dwu_ref, dwd_ref, buf, done_sem, sem):
    steps = x_ref.shape[1] // bw
    stores = [pltpu.make_async_copy(src, dst, done_sem.at[i]) for i, (src, dst) in enumerate(
        ((dwd_vmem, dwd_ref), (dwu_vmem, dwu_ref), (dx_vmem, dx_ref)))]
    for cp in stores:
        cp.start()
    for i in range(steps):
        part = slice(i * bw, (i + 1) * bw)
        buf[part] = jnp.dot(x_ref[:, part].T, dug_ref[...], preferred_element_type=F32)
        stores.append(pltpu.make_async_copy(buf.at[part], dwg_ref.at[part], sem.at[i]))
        stores[-1].start()
    for cp in stores:
        cp.wait()


def solution(mesh):
    n = mesh.shape["tp"]
    nz = n // CORES

    def local(x, dy, wg, wu, wd):
        x, dy, wg, wu, wd = (pltpu.with_memory_space_constraint(v, pltpu.HBM) for v in (x, dy, wg, wu, wd))
        rows, width = x.shape
        hid = wg.shape[1]
        tok = rows * n
        far = nz // 2
        pw = width // PIECES
        S = jax.ShapeDtypeStruct
        hbm = pl.BlockSpec(memory_space=pltpu.HBM)
        dma = pltpu.SemaphoreType.DMA
        vmem = pl.BlockSpec(memory_space=pltpu.VMEM)
        dx, xg, dug, dwu, dwd = pl.pallas_call(
            functools.partial(_main_kernel, nz, rows),
            out_shape=[S((rows, width), BF16), S((nz, CORES, rows, width), BF16),
                       S((nz, CORES * rows, hid), BF16), S((width, hid), F32), S((hid, width), F32)],
            in_specs=[hbm] * 5,
            out_specs=[vmem] * 5,
            scratch_shapes=[
                pltpu.VMEM((nz, CORES, rows, width), BF16),
                pltpu.VMEM((nz, CORES * rows, hid), BF16),
                pltpu.VMEM((nz, CORES * rows, hid), BF16),
                pltpu.VMEM((hid, tok), BF16),
                pltpu.VMEM((width, hid), BF16),
                pltpu.VMEM((width, hid), BF16),
                pltpu.VMEM((hid, width), BF16),
                pltpu.VMEM((hid, width), BF16),
                pltpu.VMEM((hid, width), BF16),
                pltpu.VMEM((width, hid), BF16),
                pltpu.VMEM((nz, PIECES // 2, CORES * rows, pw), F32),
                pltpu.VMEM((nz, PIECES // 2, CORES * rows, pw), BF16),
                pltpu.VMEM((nz, PIECES // 2, CORES * rows, pw), BF16),
                pltpu.VMEM((PIECES, rows, pw), F32),
                pltpu.VMEM((PIECES, rows, pw), BF16),
                pltpu.VMEM((PIECES, rows, pw), BF16),
                pltpu.VMEM((2, PIECES // 2, far, CORES * rows, pw), BF16),
                pltpu.VMEM((2, PIECES // 2, far, CORES * rows, pw), BF16),
                pltpu.VMEM((2, PIECES, rows, pw), BF16),
                dma((2,)), dma((3,)),
                dma((2, 2, far)), dma((2, 2, far)),
                dma((2, nz)), dma((2, nz)),
                dma((nz, PIECES // 2)), dma((nz, PIECES // 2)),
                dma((PIECES,)), dma((PIECES,)),
                dma((2, PIECES // 2, far)), dma((2, PIECES // 2, far)),
                dma((2, PIECES // 2, CORES)), dma((2, PIECES)),
            ],
            compiler_params=pltpu.CompilerParams(
                collective_id=0, has_side_effects=True, vmem_limit_bytes=36 * 1024 * 1024),
            cost_estimate=pl.CostEstimate(
                flops=2 * 5 * tok * width * hid, bytes_accessed=6 * width * hid, transcendentals=tok * hid),
            name="gather_compute_scatter",
        )(x, dy, wg, wu, wd)
        bw = 512
        dx, dwg, dwu, dwd = pl.pallas_call(
            functools.partial(_grad_kernel, bw),
            out_shape=[S((rows, width), BF16), S((width, hid), F32), S((width, hid), F32), S((hid, width), F32)],
            in_specs=[vmem] * 5,
            out_specs=[hbm] * 4,
            scratch_shapes=[pltpu.VMEM((width, hid), F32), dma((3,)), dma((width // bw,))],
            compiler_params=pltpu.CompilerParams(vmem_limit_bytes=16 * 1024 * 1024),
            cost_estimate=pl.CostEstimate(
                flops=2 * tok * width * hid, bytes_accessed=12 * width * hid, transcendentals=0),
            name="weight_grads",
        )(xg.reshape(tok, width), dug.reshape(tok, hid), dx, dwu, dwd)
        return dx, dwg, dwu, dwd

    rows = P(("dp", "tp"), None)
    return jax.shard_map(local, mesh=mesh,
                         in_specs=(rows, rows, P(None, "tp"), P(None, "tp"), P("tp", None)),
                         out_specs=(rows, P("dp", "tp"), P("dp", "tp"), rows),
                         check_vma=False)
```

time: 73.2 us -> 72.4 us (0.989)
  Pallas kernels: 72.3 us -> 71.5 us
    pallas_call x1, Pallas kernels: 65.1 us -> 64.3 us  [local(): pl.pallas_call(functools.partial(_main_kernel, nz, rows), out_shape=[S((r...]
where the time goes in v3:
time: 72.4 us; the launch traced here: 72.3 us
  Pallas kernels  71.5 us (99%)
  between operations  0.8 us (1%)
    pallas_call x1, Pallas kernels, local(): pl.pallas_call(functools.partial(_main_kernel, nz, rows), out_shape=[S((r...  64.3 us
    pallas_call x1, Pallas kernels, local(): pl.pallas_call(functools.partial(_grad_kernel, bw), out_shape=[S((rows, w...  7.21 us

profile of v3, /device:TPU:21, one launch (start us, length us, event | category | flops | bytes accessed | tf_op | source)
XLA Modules:
  0.0 72.3 jit_solution(6448948794079244641)
XLA Ops:
  0.6 64.3 %gather_compute_scatter.1 = (bf16[32,3072]{1,0:T(8,128)(2,1)S(1)}, bf16[8,2,32,3072]{3,2,1,0:T(8,128)(2,1)S(1)}, bf16[8,64,512]{2,1,0:T(8,128)(2,1)S(1)}, f32[3072,512]{1,0:T(8,128)S(1)}, f32[512,3072]{1,0:T(8,128)S(1)}) custom-call(bf16[32,3072]{1,0:T(8,128)(2,1)} %x_hbm.1, bf16[32,3072]{1,0:T(8,128)(2,1)} %dy_hbm.1, bf16[3072,512]{1,0:T(8,128)(2,1)} %wg_hbm.1, ...), custom_call_target="tpu_custom_call" | custom-call | flops 8053063680 | bytes 9437184 | tf_op jit(solution)/shard_map/gather_compute_scatter/pallas_call | solution.py:327
  65.0 7.2 %weight_grads.1 = (bf16[32,3072]{1,0:T(8,128)(2,1)}, f32[3072,512]{1,0:T(8,128)}, f32[3072,512]{1,0:T(8,128)}, f32[512,3072]{1,0:T(8,128)}) custom-call(bf16[512,3072]{1,0:T(8,128)(2,1)S(1)} %bitcast.2, bf16[512,512]{1,0:T(8,128)(2,1)S(1)} %bitcast.3, bf16[32,3072]{1,0:T(8,128)(2,1)S(1)} %get-tuple-element.11.dx_vmem, ...), custom_call_target="tpu_custom_call" | custom-call | flops 1610612736 | bytes 18874368 | tf_op jit(solution)/shard_map/weight_grads/pallas_call | solution.py:368

commit v4 on v3

--- a/solution.py
+++ b/solution.py
@@ -51,8 +51,6 @@
                for i, (src, dst) in enumerate(((wg_hbm, wg), (wu_hbm, wu), (wd_hbm, wd)))]
     for cp in own:
         cp.start()
-    for cp in wcopies:
-        cp.start()
     barrier = pltpu.get_barrier_semaphore()
     peers = [dev(0, 1 - c), dev(1, c), dev(-1, c), dev(1, 1 - c), dev(-1, 1 - c)]
     for peer in peers:
@@ -106,15 +104,18 @@
         for i, o in enumerate(offs):
             ref[o] = v[i * blk:(i + 1) * blk]
 
+    def distinct(offs):
+        return offs[:1] if offs[0] is offs[-1] else offs
+
     def x_part(offs):
-        for o in offs:
+        for o in distinct(offs):
             sib_wait(0, o)
         xb = stack(xg, offs)
         unstack(dug, offs, jnp.dot(xb, wg[...], preferred_element_type=F32).astype(BF16))
         unstack(duu, offs, jnp.dot(xb, wu[...], preferred_element_type=F32).astype(BF16))
 
     def y_part(offs, kind):
-        for o in offs:
+        for o in distinct(offs):
             sib_wait(1, o)
         g = jnp.dot(stack(dyg, offs), wdt[...], preferred_element_type=F32)
         ug = stack(dug, offs).astype(F32)
@@ -134,8 +135,8 @@
                 own_send[q] = jnp.where(c == 0, p[rows:], p[:rows]).astype(BF16)
                 own_copy(q).start()
             elif kind == "far":
-                pown[kept(FAR, q)] = p
-                psend[kept(FAR, q)] = p.astype(BF16)
+                pown[kept(FAR, q)] = p[:blk]
+                psend[kept(FAR, q)] = p[:blk].astype(BF16)
 
                 @pl.when(c == 0)
                 def _():
@@ -203,6 +204,8 @@
         for d in range(2):
             ag_copy(a, d, 1).start()
         sib_copy(a, 0).start()
+    for cp in wcopies:
+        cp.start()
     for cp, w, wt in zip(wcopies, (wg, wu, wd), (wgt, wut, wdt)):
         cp.wait()
         wt[...] = w[...].T
@@ -243,12 +246,12 @@
     y_part([near, nz - near], "pair")
     far_event(1)
 
-    x_part([far])
+    x_part([far, far])
 
     @pl.when(c == 0)
     def _():
         rs_round(0, near)
-    y_part([far], "far")
+    y_part([far, far], "far")
 
     @pl.when(c == 1)
     def _():
@@ -364,7 +367,7 @@
                 flops=2 * 5 * tok * width * hid, bytes_accessed=6 * width * hid, transcendentals=tok * hid),
             name="gather_compute_scatter",
         )(x, dy, wg, wu, wd)
-        bw = 512
+        bw = 1024
         dx, dwg, dwu, dwd = pl.pallas_call(
             functools.partial(_grad_kernel, bw),
             out_shape=[S((rows, width), BF16), S((width, hid), F32), S((width, hid), F32), S((hid, width), F32)],

time: 72.4 us -> 69.9 us (0.965)
  Pallas kernels: 71.5 us -> 69 us
    pallas_call x1, Pallas kernels: 64.3 us -> 62.4 us  [local(): pl.pallas_call(functools.partial(_main_kernel, nz, rows), out_shape=[S((r...]
where the time goes in v4:
time: 69.9 us; the launch traced here: 69.8 us
  Pallas kernels  69 us (99%)
  between operations  0.8 us (1%)
    pallas_call x1, Pallas kernels, local(): pl.pallas_call(functools.partial(_main_kernel, nz, rows), out_shape=[S((r...  62.4 us
    pallas_call x1, Pallas kernels, local(): pl.pallas_call(functools.partial(_grad_kernel, bw), out_shape=[S((rows, w...  6.66 us

profile of v4, /device:TPU:21, one launch (start us, length us, event | category | flops | bytes accessed | tf_op | source)
XLA Modules:
  0.0 69.8 jit_solution(4734522994047916305)
XLA Ops:
  0.6 62.4 %gather_compute_scatter.1 = (bf16[32,3072]{1,0:T(8,128)(2,1)S(1)}, bf16[8,2,32,3072]{3,2,1,0:T(8,128)(2,1)S(1)}, bf16[8,64,512]{2,1,0:T(8,128)(2,1)S(1)}, f32[3072,512]{1,0:T(8,128)S(1)}, f32[512,3072]{1,0:T(8,128)S(1)}) custom-call(bf16[32,3072]{1,0:T(8,128)(2,1)} %x_hbm.1, bf16[32,3072]{1,0:T(8,128)(2,1)} %dy_hbm.1, bf16[3072,512]{1,0:T(8,128)(2,1)} %wg_hbm.1, ...), custom_call_target="tpu_custom_call" | custom-call | flops 8053063680 | bytes 9437184 | tf_op jit(solution)/shard_map/gather_compute_scatter/pallas_call | solution.py:330
  63.0 6.7 %weight_grads.1 = (bf16[32,3072]{1,0:T(8,128)(2,1)}, f32[3072,512]{1,0:T(8,128)}, f32[3072,512]{1,0:T(8,128)}, f32[512,3072]{1,0:T(8,128)}) custom-call(bf16[512,3072]{1,0:T(8,128)(2,1)S(1)} %bitcast.2, bf16[512,512]{1,0:T(8,128)(2,1)S(1)} %bitcast.3, bf16[32,3072]{1,0:T(8,128)(2,1)S(1)} %get-tuple-element.11.dx_vmem, ...), custom_call_target="tpu_custom_call" | custom-call | flops 1610612736 | bytes 18874368 | tf_op jit(solution)/shard_map/weight_grads/pallas_call | solution.py:371

commit v5 on v4

--- a/solution.py
+++ b/solution.py
@@ -141,6 +141,11 @@
                 @pl.when(c == 0)
                 def _():
                     psum_copy(FAR, q).start()
+
+                if q > 0:
+                    @pl.when(c == 1)
+                    def _():
+                        rs_message((q - 1) % 2, q - 1, 0, far)
             else:
                 first = c if q % 2 == 0 else 1 - c
                 keep_o = offs[1] + first * (offs[0] - offs[1])
@@ -162,24 +167,26 @@
             rsend.at[d, q // 2, hops(d, q) - 1, pl.ds(h * rows, rows)], fin.at[d, q],
             fin_send.at[d, q // 2, h], fin_recv.at[d, q], device_id=dev(step_of(d), h), device_id_type=MESH)
 
+    def rs_message(d, q, s, n):
+        o = (n - s if d == 0 else s - n) % nz
+        o = FAR if o == far else o
+        psum_copy(o, q).wait_recv()
+        t = pown[kept(o, q)] + psib[kept(o, q)].astype(F32)
+        if s > 0:
+            rs_copy(d, q, s - 1).wait_recv()
+            t = t + rrecv[d, q // 2, s - 1].astype(F32)
+        rsend[d, q // 2, s] = t.astype(BF16)
+        if s < n - 1:
+            rs_copy(d, q, s).start()
+        else:
+            for h in range(CORES):
+                fin_copy(d, q, h).start()
+
     def rs_round(s, n):
         for q in range(PIECES):
             for d in range(2):
-                if hops(d, q) != n:
-                    continue
-                o = (n - s if d == 0 else s - n) % nz
-                o = FAR if o == far else o
-                psum_copy(o, q).wait_recv()
-                t = pown[kept(o, q)] + psib[kept(o, q)].astype(F32)
-                if s > 0:
-                    rs_copy(d, q, s - 1).wait_recv()
-                    t = t + rrecv[d, q // 2, s - 1].astype(F32)
-                rsend[d, q // 2, s] = t.astype(BF16)
-                if s < n - 1:
-                    rs_copy(d, q, s).start()
-                else:
-                    for h in range(CORES):
-                        fin_copy(d, q, h).start()
+                if hops(d, q) == n:
+                    rs_message(d, q, s, n)
 
     def rs_drain(n):
         for d in range(2):
@@ -256,7 +263,10 @@
     @pl.when(c == 1)
     def _():
         for s in range(far):
-            rs_round(s, far)
+            if s > 0:
+                rs_round(s, far)
+            else:
+                rs_message((PIECES - 1) % 2, PIECES - 1, 0, far)
             if s < far - 1:
                 grad_chunk(s, far - 1)
         rs_drain(far)

time: 69.9 us -> 69.5 us (level)
  no operation moved by 1% of the time
where the time goes in v5:
time: 69.5 us; the launch traced here: 69.4 us
  Pallas kernels  68.6 us (99%)
  between operations  0.8 us (1%)
    pallas_call x1, Pallas kernels, local(): pl.pallas_call(functools.partial(_main_kernel, nz, rows), out_shape=[S((r...  62 us
    pallas_call x1, Pallas kernels, local(): pl.pallas_call(functools.partial(_grad_kernel, bw), out_shape=[S((rows, w...  6.66 us

profile of v5, /device:TPU:21, one launch (start us, length us, event | category | flops | bytes accessed | tf_op | source)
XLA Modules:
  0.0 69.4 jit_solution(6119214146240909752)
XLA Ops:
  0.6 62.0 %gather_compute_scatter.1 = (bf16[32,3072]{1,0:T(8,128)(2,1)S(1)}, bf16[8,2,32,3072]{3,2,1,0:T(8,128)(2,1)S(1)}, bf16[8,64,512]{2,1,0:T(8,128)(2,1)S(1)}, f32[3072,512]{1,0:T(8,128)S(1)}, f32[512,3072]{1,0:T(8,128)S(1)}) custom-call(bf16[32,3072]{1,0:T(8,128)(2,1)} %x_hbm.1, bf16[32,3072]{1,0:T(8,128)(2,1)} %dy_hbm.1, bf16[3072,512]{1,0:T(8,128)(2,1)} %wg_hbm.1, ...), custom_call_target="tpu_custom_call" | custom-call | flops 8053063680 | bytes 9437184 | tf_op jit(solution)/shard_map/gather_compute_scatter/pallas_call | solution.py:340
  62.6 6.7 %weight_grads.1 = (bf16[32,3072]{1,0:T(8,128)(2,1)}, f32[3072,512]{1,0:T(8,128)}, f32[3072,512]{1,0:T(8,128)}, f32[512,3072]{1,0:T(8,128)}) custom-call(bf16[512,3072]{1,0:T(8,128)(2,1)S(1)} %bitcast.2, bf16[512,512]{1,0:T(8,128)(2,1)S(1)} %bitcast.3, bf16[32,3072]{1,0:T(8,128)(2,1)S(1)} %get-tuple-element.11.dx_vmem, ...), custom_call_target="tpu_custom_call" | custom-call | flops 1610612736 | bytes 18874368 | tf_op jit(solution)/shard_map/weight_grads/pallas_call | solution.py:381
